TPU v7x, 32 devices: a whole 2x2x4 slice. The times are simulated.
32 devices in a mesh: samp: 4 (over y, x), snp: 8 (over z, core).
Axes of the slice: x: 2, y: 2, z: 4, core: 2. Of those that a mesh axis runs over, the one named last changes fastest.
Arguments:
- genotypes: int32 [8192, 8192], P('samp', 'snp'), may hold values from 0 to 2
- win_lo: int32 [8192], P('snp'), may hold values from 0 to 8191, as said below
- win_hi: int32 [8192], P('snp'), may hold values from 0 to 8191, as said below
- annotation: int32 [8192], P('snp'), may hold values from 0 to 127
- chromosome: int32 [8192], P('snp'), may hold values from 0 to 21, never falling along the last dimension, each value on 1 to 512 neighbouring positions
- chi_square: float32 [8192], P('snp'), may hold values from 0.3 to 60
Outputs:
- annotation_scores: float32 [128, 8192], P('snp')
- gram: float32 [128, 128], replicated
- moments: float32 [2, 128], replicated
- totals: float32 [2], replicated
Inputs may be any that keep to these rules, and one draw needn't show every extreme that they name: i - 512 <= win_lo[i] <= i, nondecreasing in i; the distance 512 is reached. i <= win_hi[i] <= i + 512, nondecreasing in i; the distance 512 is reached.
All inputs are finite; a program needn't handle non-finite values.
Results may differ from a plain program's by a relative error of at most 0.0003.
The roundings to bfloat16 on the way count: a program that leaves them out, or rounds other values in their place, can miss the bound.
Values may be sent and summed in bfloat16 or wider, within the bound.
A program may use at most 64 MiB of HBM per device.

v0:
```python
import jax
import jax.numpy as jnp
from jax import lax
from jax.sharding import PartitionSpec as P

A = 128


def extended(cells, sides, width):
    for axis, dim in sides:
        count = lax.axis_size(axis)
        ends = count - 1
        head = lax.slice_in_dim(cells, 0, width, axis=dim)
        tail = lax.slice_in_dim(cells, cells.shape[dim] - width, cells.shape[dim], axis=dim)
        cells = jnp.concatenate(
            [
                lax.ppermute(tail, axis, [(i, (i + 1) % count) for i in range(ends)]),
                cells,
                lax.ppermute(head, axis, [((i + 1) % count, i) for i in range(ends)]),
            ],
            axis=dim,
        )
    return cells


def body(genotypes, win_lo, win_hi, annotation, chromosome, chi_square):
    samp_rows, block_cols = genotypes.shape
    reach = block_cols // 2
    samp_count = lax.axis_size("samp")
    total_samples = samp_rows * samp_count
    dosage = genotypes.astype(jnp.float32)
    dose_sums, dose_squares = lax.psum((jnp.sum(dosage, 0), jnp.sum(dosage * dosage, 0)), "samp")
    mean_dose = dose_sums / total_samples
    variance = dose_squares / total_samples - mean_dose * mean_dose
    standard = ((dosage - mean_dose) * lax.rsqrt(variance + 1e-05)).astype(jnp.bfloat16)
    first_snp = lax.axis_index("snp") * block_cols
    labels = jnp.arange(A, dtype=jnp.int32)
    own_labels = jnp.stack([annotation, chromosome]).astype(jnp.bfloat16)
    wide_z, wide_labels = (
        extended(standard, (("snp", 1),), reach),
        extended(own_labels, (("snp", 1),), reach),
    )
    annot_wide = wide_labels[0].astype(jnp.int32)
    chrom_wide = wide_labels[1].astype(jnp.int32)
    span = wide_z.shape[1] - block_cols + reach

    def tile_piece(row_start, count):
        band = row_start // reach * reach
        rows_z = lax.dynamic_slice_in_dim(standard, row_start, count, 1)
        cols_z = lax.dynamic_slice_in_dim(wide_z, band, span, 1)
        return lax.dot_general(
            rows_z, cols_z, (((0,), (0,)), ((), ())), preferred_element_type=jnp.float32
        )

    share = block_cols // samp_count
    row_start = jnp.int32(0)
    tile = lax.psum_scatter(
        jnp.concatenate(
            [
                tile_piece(row_start + offset * share, share)
                for offset in range(share * lax.axis_size("samp") // share)
            ],
            0,
        ),
        "samp",
        scatter_dimension=0,
        tiled=True,
    )
    row_begin = lax.axis_index("samp") * share
    row_start = row_begin + 0
    band = row_start // reach * reach
    corr = tile / total_samples
    square = corr * corr
    adjusted = square - (1.0 - square) / (total_samples - 2)
    col_ids = first_snp + band - reach + jnp.arange(span, dtype=jnp.int32)
    lower_end = lax.dynamic_slice_in_dim(win_lo, row_start, share)
    upper_end = lax.dynamic_slice_in_dim(win_hi, row_start, share)
    chrom_rows = lax.dynamic_slice_in_dim(chromosome, row_start, share)
    chrom_cols = lax.dynamic_slice_in_dim(chrom_wide, band, span)
    annot_cols = lax.dynamic_slice_in_dim(annot_wide, band, span)
    inside = (col_ids[None, :] >= lower_end[:, None]) & (col_ids[None, :] <= upper_end[:, None])
    inside = inside & (chrom_cols[None, :] == chrom_rows[:, None])
    kept = jnp.where(inside, adjusted, 0.0)
    member = (annot_cols[:, None] == labels[None, :]).astype(jnp.float32)
    part_scores = lax.dot_general(
        member,
        kept,
        (((0,), (1,)), ((), ())),
        precision=lax.Precision.HIGHEST,
        preferred_element_type=jnp.float32,
    )
    scores = lax.all_gather(part_scores, "samp", axis=1, tiled=True)
    weights = 1.0 / jnp.sum(scores, 0)
    weighted = scores * weights[None, :]
    gram_part = lax.dot_general(
        weighted,
        scores,
        (((1,), (1,)), ((), ())),
        precision=lax.Precision.HIGHEST,
        preferred_element_type=jnp.float32,
    )
    moment_part = jnp.stack([jnp.sum(weighted, 1), jnp.sum(weighted * chi_square[None, :], 1)])
    total_part = jnp.stack([jnp.sum(weights), jnp.sum(weights * chi_square)])
    gram, moments, totals = lax.psum((gram_part, moment_part, total_part), "snp")
    snp_total = block_cols * lax.axis_size("snp")
    scale = A / snp_total
    regrouped = lax.all_to_all(scores, "snp", split_axis=0, concat_axis=1, tiled=True)
    return (regrouped, scale * gram, scale * moments, totals / snp_total)


def solution(mesh):
    in_specs = (P("samp", "snp"), P("snp"), P("snp"), P("snp"), P("snp"), P("snp"))
    out_specs = (P("snp", None), P(), P(), P())
    return jax.shard_map(body, mesh=mesh, in_specs=in_specs, out_specs=out_specs, check_vma=False)
```

profile of v0, /device:TPU:0, one launch (start us, length us, event | category | flops | bytes accessed | tf_op | source)
XLA Modules:
  0.0 220.2 jit_solution(12471998760176331040)
XLA Ops:
  7.2 4.5 %convert_reduce_fusion = (f32[1024]{0:T(1024)S(1)}, f32[1024]{0:T(1024)S(1)}) fusion(s32[2048,1024]{1,0:T(8,128)} %param.6), kind=kLoop, calls=%fused_computation.2 | loop fusion | flops 8386560 | bytes 8396800 | tf_op jit(solution)/shard_map/reduce_sum | solution.py:32
  11.7 11.5 %all-reduce.1 = (f32[1024]{0:T(1024)S(1)}, f32[1024]{0:T(1024)S(1)}) all-reduce(f32[1024]{0:T(1024)S(1)} %get-tuple-element.5, f32[1024]{0:T(1024)S(1)} %get-tuple-element.4), channel_id=1, replica_groups=mesh['samp'=4,'snp'=8] {'samp'}, use_global_device_ids=true, to_apply=%region_3.0 | all-reduce | flops 2048 | bytes 16384 | tf_op jit(solution)/shard_map/psum | solution.py:32
  23.3 4.7 %multiply_convert_fusion = bf16[2048,1024]{1,0:T(8,128)(2,1)S(1)} fusion(s32[2048,1024]{1,0:T(8,128)} %param.6, f32[1024]{0:T(1024)S(1)} %get-tuple-element.22, f32[1024]{0:T(1024)S(1)} %get-tuple-element.21), kind=kLoop, calls=%fused_computation | loop fusion | flops 8388608 | bytes 12591104 | tf_op jit(solution)/shard_map/convert_element_type | solution.py:35
  28.3 1.4 collective-permute-start.2
  29.8 1.3 collective-permute-start.3
  31.1 2.3 %collective-permute-done.2 = bf16[2048,512]{1,0:T(8,128)(2,1)S(1)} collective-permute-done((bf16[2048,512]{1,0:T(8,128)(2,1)S(1)}, bf16[2048,512]{1,0:T(8,128)(2,1)S(1)}, u32[]{:S(2)}, u32[]{:S(2)}) %collective-permute-start.2) | collective-permute-done | bytes 2097184 | tf_op jit(solution)/shard_map/ppermute | solution.py:17
  33.4 1.8 fusion.2
  35.2 1.8 fusion.3
  37.5 1.8 fusion.1
  39.3 1.8 fusion
  41.1 2.9 %pad_maximum_fusion.2 = f32[1024,1536]{1,0:T(8,128)} fusion(f32[256,1536]{1,0:T(8,128)S(1)} %fusion, f32[256,1536]{1,0:T(8,128)S(1)} %fusion.1, f32[256,1536]{1,0:T(8,128)S(1)} %fusion.2, f32[256,1536]{1,0:T(8,128)S(1)} %fusion.3), kind=kLoop, calls=%fused_computation.5 | loop fusion | flops 4718592 | bytes 12582912 | tf_op jit(solution)/shard_map/concatenate | solution.py:58
  44.8 23.7 %collective-permute-start = (bf16[2,512]{1,0:T(2,128)(2,1)S(1)}, bf16[2,512]{1,0:T(2,128)(2,1)S(1)}, u32[]{:S(2)}, u32[]{:S(2)}) collective-permute-start(bf16[2,512]{1,0:T(2,128)(2,1)S(1)} %get-tuple-element.18), channel_id=1, source_target_pairs={{0,1},{1,2},{2,3},{3,4},{4,5},{5,6},{6,7},{8,9},{9,10},{10,11},{11... | collective-permute-start | bytes 6152 | tf_op jit(solution)/shard_map/ppermute | solution.py:17
  68.5 1.3 collective-permute-start.1
  71.4 1.4 collective-permute-done.1
  72.9 62.5 %reduce-scatter.2.cloned.1.call-done = f32[256,1536]{1,0:T(8,128)} async-done(((f32[1024,1536]{1,0:T(8,128)}), f32[256,1536]{1,0:T(8,128)}) %reduce-scatter.2.cloned.1.call-update) | async-done | bytes 1572880 | tf_op jit(solution)/shard_map/reduce_scatter | solution.py:57
  135.5 3.0 %fusion.4 = f32[128,256]{1,0:T(8,128)S(1)} fusion(f32[256,1536]{1,0:T(8,128)} %reduce-scatter.2.cloned.1.call-done, s32[1536]{0:T(1024)S(1)} %get-tuple-element.23, s32[1536]{0:T(1024)S(1)} %iota_add_fusion, s32[256]{0:T(256)S(1)} %dynamic_slice.41, s32[256]{0:T(256)S(1)} %dynamic_slice.38, s32[256]{0:T(256)S(1)} %dynamic_slice.37, ...), kind=kOutput, calls=%fused_computation.10 | convolution fusion | flops 608698368 | bytes 1725440 | tf_op jit(solution)/shard_map/dot_general | solution.py:85
  138.5 10.6 %all_gather.3 = f32[128,1024]{1,0:T(8,128)} all-gather(f32[128,256]{1,0:T(8,128)S(1)} %fusion.4), channel_id=1, replica_groups=mesh['samp'=4,'snp'=8] {'samp'}, dimensions={1}, use_global_device_ids=true | all-gather | bytes 655360 | tf_op jit(solution)/shard_map/all_gather | solution.py:92
  150.8 2.4 %fusion.30 = f32[128,128]{1,0:T(8,128)} fusion(f32[128,1024]{1,0:T(8,128)} %all_gather.3, f32[1024]{0:T(1024)S(1)} %get-tuple-element.20), kind=kOutput, calls=%fused_computation.39 | convolution fusion | flops 201457664 | bytes 593920 | tf_op jit(solution)/shard_map/dot_general | solution.py:95
  153.3 4.6 %all-to-all-start = ((f32[8,16,1024]{2,1,0:T(8,128)}), f32[8,16,1024]{2,1,0:T(8,128)S(1)}, u32[]{:S(2)}, u32[]{:S(2)}) async-start(f32[8,16,1024]{2,1,0:T(8,128)} %bitcast), calls=%async_computation.1 | async-start | bytes 1048576 | tf_op jit(solution)/shard_map/all_to_all | solution.py:107
  157.9 1.4 pad_maximum_fusion.10
  159.3 1.2 multiply_reduce_fusion.1
  160.5 18.6 %all-reduce = (f32[2,128]{1,0:T(2,128)S(1)}, f32[2]{0:T(128)S(1)}) all-reduce(f32[2,128]{1,0:T(2,128)S(1)} %pad_maximum_fusion.9, f32[2]{0:T(128)S(1)} %pad_maximum_fusion.10), channel_id=1, replica_groups=mesh['samp'=4,'snp'=8] {'snp'}, use_global_device_ids=true, to_apply=%region_9.10 | all-reduce | flops 258 | bytes 2064 | tf_op jit(solution)/shard_map/psum | solution.py:104
  180.1 30.9 %all-reduce.4.cloned.1.call-done = f32[128,128]{1,0:T(8,128)} async-done(((f32[128,128]{1,0:T(8,128)}), f32[128,128]{1,0:T(8,128)}) %all-reduce.4.cloned.1.call-update) | async-done | bytes 65552 | tf_op jit(solution)/shard_map/psum | solution.py:104
  211.1 1.5 broadcast_multiply_fusion
  (33 shorter events, 6.8 us)
Async XLA Ops:
  7.2 128.3 %reduce-scatter.2.cloned.1.call-start = ((), (), s32[]{:S(2)}) async-start(), calls=%async_computation.2 | async-start | bytes 7864320 | tf_op jit(solution)/shard_map/reduce_scatter | solution.py:57
  28.3 5.1 %collective-permute-start.2 = (bf16[2048,512]{1,0:T(8,128)(2,1)S(1)}, bf16[2048,512]{1,0:T(8,128)(2,1)S(1)}, u32[]{:S(2)}, u32[]{:S(2)}) collective-permute-start(bf16[2048,512]{1,0:T(8,128)(2,1)S(1)} %get-tuple-element.14), channel_id=1, source_target_pairs={{0,1},{1,2},{2,3},{3,4},{4,5},{5,6},{6,7},{8,9},{9,10},{10,11},{11... | collective-permute-start | bytes 6291464 | tf_op jit(solution)/shard_map/ppermute | solution.py:17
  29.8 7.7 %collective-permute-start.3 = (bf16[2048,512]{1,0:T(8,128)(2,1)S(1)}, bf16[2048,512]{1,0:T(8,128)(2,1)S(1)}, u32[]{:S(2)}, u32[]{:S(2)}) collective-permute-start(bf16[2048,512]{1,0:T(8,128)(2,1)S(1)} %get-tuple-element.15), channel_id=1, source_target_pairs={{1,0},{2,1},{3,2},{4,3},{5,4},{6,5},{7,6},{9,8},{10,9},{11,10},{12... | collective-permute-start | bytes 6291464 | tf_op jit(solution)/shard_map/ppermute | solution.py:19
  44.0 0.7 copy-start.2
  44.0 0.7 copy-start.1
  44.1 106.2 %copy-start = (f32[1024]{0:T(1024)S(1)}, f32[1024]{0:T(1024)}, u32[]{:S(2)}) copy-start(f32[1024]{0:T(1024)} %param.11) | copy-start | bytes 12292
  44.1 167.0 %all-reduce.4.cloned.1.call-start = ((), (), s32[]{:S(2)}) async-start(), calls=%async_computation.3 | async-start | bytes 131072 | tf_op jit(solution)/shard_map/psum | solution.py:104
  44.8 26.6 %collective-permute-start = (bf16[2,512]{1,0:T(2,128)(2,1)S(1)}, bf16[2,512]{1,0:T(2,128)(2,1)S(1)}, u32[]{:S(2)}, u32[]{:S(2)}) collective-permute-start(bf16[2,512]{1,0:T(2,128)(2,1)S(1)} %get-tuple-element.18), channel_id=1, source_target_pairs={{0,1},{1,2},{2,3},{3,4},{4,5},{5,6},{6,7},{8,9},{9,10},{10,11},{11... | collective-permute-start | bytes 6152 | tf_op jit(solution)/shard_map/ppermute | solution.py:17
  68.5 4.3 %collective-permute-start.1 = (bf16[2,512]{1,0:T(2,128)(2,1)S(1)}, bf16[2,512]{1,0:T(2,128)(2,1)S(1)}, u32[]{:S(2)}, u32[]{:S(2)}) collective-permute-start(bf16[2,512]{1,0:T(2,128)(2,1)S(1)} %get-tuple-element.19), channel_id=1, source_target_pairs={{1,0},{2,1},{3,2},{4,3},{5,4},{6,5},{7,6},{9,8},{10,9},{11,10},{12... | collective-permute-start | bytes 6152 | tf_op jit(solution)/shard_map/ppermute | solution.py:19
  153.3 59.3 %all-to-all-start = ((f32[8,16,1024]{2,1,0:T(8,128)}), f32[8,16,1024]{2,1,0:T(8,128)S(1)}, u32[]{:S(2)}, u32[]{:S(2)}) async-start(f32[8,16,1024]{2,1,0:T(8,128)} %bitcast), calls=%async_computation.1 | async-start | bytes 1048576 | tf_op jit(solution)/shard_map/all_to_all | solution.py:107
Sparse Core Ops, SparseCore 0:
  44.2 91.2 reduce-scatter.1
  153.4 57.6 all-reduce.3
where the time goes:
time: 221 us; the launch traced here: 220 us
  waiting for transfers between devices  97.7 us (44%)
  blocking collectives  40.8 us (18%)
  starting transfers between devices  32.4 us (15%)
  other arithmetic  19 us (9%)
  between operations  14.2 us (6%)
  matrix products  12.7 us (6%)
  local copies, waits for them, and re-layouts  3.39 us (2%)
    reduce_scatter x1, waiting for transfers between devices, body(): lax.psum_scatter(jnp.concatenate([tile_piece(row_start + offset * share,...  62.5 us
    psum x1, waiting for transfers between devices, body(): lax.psum((gram_part, moment_part, total_part), 'snp')  30.9 us
    ppermute x2, starting transfers between devices, extended(): lax.ppermute(tail, axis, [(i, (i + 1) % count) for i in range(ends)])  25.1 us
    psum x1, blocking collectives, body(): lax.psum((gram_part, moment_part, total_part), 'snp')  18.6 us
    psum x1, blocking collectives, body(): lax.psum((jnp.sum(dosage, 0), jnp.sum(dosage * dosage, 0)), 'samp')  11.5 us
    all_gather x1, blocking collectives, body(): scores = lax.all_gather(part_scores, 'samp', axis=1, tiled=True)  10.6 us
    dot_general x4, matrix products, tile_piece(): lax.dot_general(rows_z, cols_z, (((0,), (0,)), ((), ())), preferred_eleme...  7.27 us
    convert_element_type x1, other arithmetic, body(): ((dosage - mean_dose) * lax.rsqrt(variance + 1e-05)).astype(jnp.bfloat16)  4.68 us
  transfers between devices with their start and end apart: 7, of which 5 were waited for; matrix products, arithmetic and copies ran while one was open for 5% of the time, Pallas kernels for 0%

commit v1 on v0

v1 whole, which is shorter than its diff:
```python
import functools

import jax
import jax.numpy as jnp
from jax import lax
from jax.experimental import pallas as pl
from jax.experimental.pallas import tpu as pltpu
from jax.sharding import PartitionSpec as P

A = 128
EDGE = 32000.0


def remote(src, dst, send_sem, recv_sem, device):
    return pltpu.make_async_remote_copy(
        src_ref=src,
        dst_ref=dst,
        send_sem=send_sem,
        recv_sem=recv_sem,
        device_id=device,
        device_id_type=pl.DeviceIdType.MESH,
    )


def kernel(
    n_samp, n_snp, chunk,
    meta_ref, geno_ref,
    out_ref, gram_ref, small_ref,
    gbuf, zt, wide, labels, stat, stat_all, own, sendq, recvq,
    score_parts, gs_parts, score_in, gs_in, gs_sum, score_all, gs_all, gram_rows, gram_all,
    load_sem, stat_ss, stat_rs, lab_ss, lab_rs, halo_ss, halo_rs, tile_ss, tile_rs,
    a1_ss, a1_rs, a2_ss, a2_rs, b1_ss, b1_rs, b2_ss, b2_rs, c_ss, c_rs,
):
    rows, cols = gbuf.shape
    half = cols // 2
    share = cols // n_samp
    tiles = recvq.shape[1]
    n_chunks = rows // chunk
    group = A // n_snp
    total = rows * n_samp
    steps = EDGE / (total * 1.004)
    s = lax.axis_index("samp")
    p = lax.axis_index("snp")
    has_left = p > 0
    has_right = p < n_snp - 1
    left = jnp.maximum(p - 1, 0)
    right = jnp.minimum(p + 1, n_snp - 1)

    def load(c):
        part = pl.ds(pl.multiple_of(c * chunk, chunk), chunk)
        return pltpu.make_async_copy(geno_ref.at[part], gbuf.at[part], load_sem.at[c])

    for c in range(n_chunks):
        load(c).start()

    barrier = pltpu.get_barrier_semaphore()
    for k in range(1, n_samp):
        pl.semaphore_signal(barrier, inc=1, device_id={"samp": lax.rem(s + k, n_samp)}, device_id_type=pl.DeviceIdType.MESH)

    @pl.loop(1, n_snp)
    def _(k):
        pl.semaphore_signal(barrier, inc=1, device_id={"snp": lax.rem(p + k, n_snp)}, device_id_type=pl.DeviceIdType.MESH)

    pl.semaphore_wait(barrier, n_samp - 1 + n_snp - 1)

    lab_left = remote(meta_ref.at[:, pl.ds(0, half)], labels.at[:, pl.ds(half + cols, half)], lab_ss.at[0], lab_rs.at[0], {"snp": left})
    lab_right = remote(meta_ref.at[:, pl.ds(half, half)], labels.at[:, pl.ds(0, half)], lab_ss.at[1], lab_rs.at[1], {"snp": right})

    @pl.when(has_left)
    def _():
        lab_left.start()

    @pl.when(has_right)
    def _():
        lab_right.start()

    def tally(c, sums):
        load(c).wait()
        one, two = sums
        for b in range(cols // 256):
            g = gbuf[pl.ds(pl.multiple_of(c * chunk, chunk), chunk), b * 256:(b + 1) * 256].astype(jnp.float32)
            g1 = jnp.sum(g.reshape(chunk // 8, 8, 256), 0)
            g2 = jnp.sum((g * g).reshape(chunk // 8, 8, 256), 0)
            one = one[:b] + (one[b] + g1,) + one[b + 1:]
            two = two[:b] + (two[b] + g2,) + two[b + 1:]
        return one, two

    blank = tuple(jnp.zeros((8, 256), jnp.float32) for _ in range(cols // 256))
    one, two = lax.fori_loop(0, n_chunks, tally, (blank, blank))
    for b in range(cols // 256):
        stat[0:1, b * 256:(b + 1) * 256] = jnp.sum(one[b], 0, keepdims=True)
        stat[1:2, b * 256:(b + 1) * 256] = jnp.sum(two[b], 0, keepdims=True)

    def stat_copy(k):
        return remote(stat, stat_all.at[k - 1], stat_ss.at[k - 1], stat_rs.at[k - 1], {"samp": lax.rem(s + k, n_samp)})

    for k in range(1, n_samp):
        stat_copy(k).start()
    labels[:, half:half + cols] = meta_ref[...]

    @pl.when(jnp.logical_not(has_left))
    def _():
        wide[:, 0:half] = jnp.zeros((rows, half), jnp.bfloat16)
        labels[:, 0:half] = jnp.full((8, half), -1.0, jnp.float32)

    @pl.when(jnp.logical_not(has_right))
    def _():
        wide[:, half + cols:] = jnp.zeros((rows, half), jnp.bfloat16)
        labels[:, half + cols:] = jnp.full((8, half), -1.0, jnp.float32)

    sums = stat[...]
    for k in range(1, n_samp):
        stat_copy(k).wait()
        sums = sums + stat_all[k - 1]
    mean = sums[0:1] / total
    scale = lax.rsqrt(sums[1:2] / total - mean * mean + 1e-05)

    def halo_left(c):
        part = pl.ds(pl.multiple_of(c * chunk, chunk), chunk)
        return remote(wide.at[part, pl.ds(half, half)], wide.at[part, pl.ds(half + cols, half)], halo_ss.at[0, c], halo_rs.at[0, c], {"snp": left})

    def halo_right(c):
        part = pl.ds(pl.multiple_of(c * chunk, chunk), chunk)
        return remote(wide.at[part, pl.ds(cols, half)], wide.at[part, pl.ds(0, half)], halo_ss.at[1, c], halo_rs.at[1, c], {"snp": right})

    def halo_start(c):
        @pl.when(has_left)
        def _():
            halo_left(c).start()

        @pl.when(has_right)
        def _():
            halo_right(c).start()

    @pl.loop(0, n_chunks)
    def _(c):
        start = pl.multiple_of(c * chunk, chunk)
        for b in range(cols // 256):
            at = slice(b * 256, (b + 1) * 256)
            g = gbuf[pl.ds(start, chunk), at].astype(jnp.float32)
            z = (g - mean[:, at]) * scale[:, at]
            wide[pl.ds(start, chunk), half + b * 256:half + (b + 1) * 256] = z.astype(jnp.bfloat16)
            zt[at, pl.ds(start, chunk)] = z.T.astype(jnp.bfloat16)

        halo_start(c)

    def tile_copy(k, t):
        return remote(sendq.at[k - 1, t], recvq.at[k - 1, t], tile_ss.at[k - 1, t], tile_rs.at[k - 1, t], {"samp": lax.rem(s + k, n_samp)})

    def tile_pass(inner):
        @pl.loop(0, n_samp * tiles)
        def _(step):
            k = lax.rem(step // tiles + 1, n_samp)
            t = lax.rem(step, tiles)
            r = lax.rem(s + k, n_samp)
            at = r * share + t * share
            inside = jnp.logical_and(at >= half, at < half + cols)

            @pl.when(inside if inner else jnp.logical_not(inside))
            def _():
                part = jnp.dot(
                    zt[pl.ds(pl.multiple_of(r * share, share), share), :],
                    wide[:, pl.ds(pl.multiple_of(at, share), share)],
                    preferred_element_type=jnp.float32,
                )

                @pl.when(k == 0)
                def _():
                    own[t] = part

                @pl.when(k > 0)
                def _():
                    fixed = jnp.clip(jnp.round(part * steps), -32767.0, 32767.0)
                    sendq[k - 1, t] = fixed.astype(jnp.int32).astype(jnp.int16)
                    tile_copy(k, t).start()

    tile_pass(True)

    @pl.when(has_left)
    def _():
        lab_left.wait_send()
        lab_right.wait_recv()

        @pl.loop(0, n_chunks)
        def _(c):
            halo_left(c).wait_send()
            halo_right(c).wait_recv()

    @pl.when(has_right)
    def _():
        lab_right.wait_send()
        lab_left.wait_recv()

        @pl.loop(0, n_chunks)
        def _(c):
            halo_right(c).wait_send()
            halo_left(c).wait_recv()

    tile_pass(False)

    mine = pl.multiple_of(s * share, share)
    info = meta_ref[:, pl.ds(mine, share)]
    turned = jnp.concatenate([info] + [jnp.zeros((A - 8, share), jnp.float32)], 0).T
    lower, upper, chrom = turned[:, 0:1], turned[:, 1:2], turned[:, 2:3]
    chi = info[4:5]
    first = (p * cols - half).astype(jnp.int32)

    def add_tile(t, scores):
        tile = own[t]
        got = jnp.zeros((share, share), jnp.float32)
        for k in range(1, n_samp):
            tile_copy(k, t).wait()
            got = got + recvq[k - 1, t].astype(jnp.int32).astype(jnp.float32)
        corr = (tile + got * (1.0 / steps)) / total
        square = corr * corr
        adjusted = square - (1.0 - square) / (total - 2)
        at = pl.multiple_of((s + t) * share, share)
        lab = labels[:, pl.ds(at, share)]
        ids = (first + at + lax.broadcasted_iota(jnp.int32, (1, share), 1)).astype(jnp.float32)
        inside = (ids >= lower) & (ids <= upper) & (lab[2:3] == chrom)
        kept = jnp.where(inside, adjusted, 0.0)
        cats = lax.broadcasted_iota(jnp.int32, (A, share), 0).astype(jnp.float32)
        member = jnp.where(cats == lab[3:4], 1.0, 0.0).astype(jnp.bfloat16)
        for _ in range(3):
            piece = kept.astype(jnp.bfloat16)
            kept = kept - piece.astype(jnp.float32)
            scores = scores + lax.dot_general(member, piece, (((1,), (1,)), ((), ())), preferred_element_type=jnp.float32)
        return scores

    scores = lax.fori_loop(0, tiles, add_tile, jnp.zeros((A, share), jnp.float32))

    weights = 1.0 / jnp.sum(scores, 0, keepdims=True)
    weighted = scores * weights
    gram = lax.dot_general(
        weighted, scores, (((1,), (1,)), ((), ())), precision=lax.Precision.HIGHEST, preferred_element_type=jnp.float32
    )
    for q in range(n_snp):
        score_parts[q] = scores[q * group:(q + 1) * group]
    pair = jnp.concatenate([weights, weights * chi, jnp.zeros((6, share), jnp.float32)], 0)
    moments = lax.dot_general(
        pair, scores, (((1,), (1,)), ((), ())), precision=lax.Precision.HIGHEST, preferred_element_type=jnp.float32
    )
    sums2 = jnp.broadcast_to(jnp.sum(pair, 1, keepdims=True), (8, A))
    for q in range(n_snp):
        gs_parts[q, 0:8] = jnp.concatenate([moments[0:2], sums2[0:2], moments[4:8]], 0)
        gs_parts[q, 8:8 + group] = gram[q * group:(q + 1) * group]

    def send_gs(k):
        q = lax.rem(p + k, n_snp)
        return remote(gs_parts.at[q], gs_in.at[k], a1_ss.at[k], a1_rs.at[k], {"snp": q})

    def send_scores(k):
        q = lax.rem(p + k, n_snp)
        return remote(score_parts.at[q], score_in.at[p], a2_ss.at[k], a2_rs.at[k], {"snp": q})

    @pl.loop(1, n_snp)
    def _(k):
        send_gs(k).start()

    @pl.loop(1, n_snp)
    def _(k):
        send_scores(k).start()

    score_in[p] = score_parts[p]

    def add_gs(k, so_far):
        send_gs(k).wait()
        return so_far + gs_in[k]

    gs_sum[...] = lax.fori_loop(1, n_snp, add_gs, gs_parts[p])

    def share_gs(k):
        return remote(gs_sum, gs_all.at[k - 1], b1_ss.at[k - 1], b1_rs.at[k - 1], {"samp": lax.rem(s + k, n_samp)})

    def share_scores(k):
        return remote(score_in, score_all.at[s], b2_ss.at[k - 1], b2_rs.at[k - 1], {"samp": lax.rem(s + k, n_samp)})

    for k in range(1, n_samp):
        share_gs(k).start()

    @pl.loop(1, n_snp)
    def _(k):
        send_scores(k).wait()

    for k in range(1, n_samp):
        share_scores(k).start()
    score_all[s] = score_in[...]

    full = gs_sum[...]
    for k in range(1, n_samp):
        share_gs(k).wait()
        full = full + gs_all[k - 1]
    gram_rows[...] = full[8:8 + group]
    factor = A / (cols * n_snp)
    small_ref[...] = full[0:8]

    def send_rows(k):
        return remote(gram_rows, gram_all.at[p], c_ss.at[k], c_rs.at[k], {"snp": lax.rem(p + k, n_snp)})

    @pl.loop(1, n_snp)
    def _(k):
        send_rows(k).start()

    gram_all[p] = gram_rows[...]

    @pl.loop(1, n_snp)
    def _(k):
        send_rows(k).wait()

    for q in range(n_snp):
        gram_ref[q * group:(q + 1) * group, :] = gram_all[q] * factor
    for k in range(1, n_samp):
        share_scores(k).wait()
    for r in range(n_samp):
        for q in range(n_snp):
            start = q * cols + r * share
            out_ref[:, start:start + share] = score_all[r, q]


def solution(mesh):
    n_samp, n_snp = mesh.shape["samp"], mesh.shape["snp"]

    def body(genotypes, win_lo, win_hi, annotation, chromosome, chi_square):
        rows, cols = genotypes.shape
        half, share = cols // 2, cols // n_samp
        chunk = 256
        n_chunks = rows // chunk
        tiles = (cols + share) // share
        group = A // n_snp
        as_row = lambda x: x.astype(jnp.float32)
        nothing = jnp.zeros((cols,), jnp.float32)
        meta = jnp.stack(
            [as_row(win_lo), as_row(win_hi), as_row(chromosome), as_row(annotation), chi_square, nothing, nothing, nothing]
        )
        f32, bf16, i16 = jnp.float32, jnp.bfloat16, jnp.int16
        dma = pltpu.SemaphoreType.DMA
        out, gram, small = pl.pallas_call(
            functools.partial(kernel, n_samp, n_snp, chunk),
            out_shape=(
                jax.ShapeDtypeStruct((group, cols * n_snp), f32),
                jax.ShapeDtypeStruct((A, A), f32),
                jax.ShapeDtypeStruct((8, A), f32),
            ),
            in_specs=[pl.BlockSpec(memory_space=pltpu.VMEM), pl.BlockSpec(memory_space=pl.ANY)],
            out_specs=(pl.BlockSpec(memory_space=pltpu.VMEM),) * 3,
            scratch_shapes=[
                pltpu.VMEM((rows, cols), jnp.int32),
                pltpu.VMEM((cols, rows), bf16),
                pltpu.VMEM((rows, 2 * cols), bf16),
                pltpu.VMEM((8, 2 * cols), f32),
                pltpu.VMEM((2, cols), f32),
                pltpu.VMEM((n_samp - 1, 2, cols), f32),
                pltpu.VMEM((tiles, share, share), f32),
                pltpu.VMEM((n_samp - 1, tiles, share, share), i16),
                pltpu.VMEM((n_samp - 1, tiles, share, share), i16),
                pltpu.VMEM((n_snp, group, share), f32),
                pltpu.VMEM((n_snp, group + 8, A), f32),
                pltpu.VMEM((n_snp, group, share), f32),
                pltpu.VMEM((n_snp, group + 8, A), f32),
                pltpu.VMEM((group + 8, A), f32),
                pltpu.VMEM((n_samp, n_snp, group, share), f32),
                pltpu.VMEM((n_samp - 1, group + 8, A), f32),
                pltpu.VMEM((group, A), f32),
                pltpu.VMEM((n_snp, group, A), f32),
                dma((n_chunks,)),
                dma((n_samp - 1,)), dma((n_samp - 1,)),
                dma((2,)), dma((2,)),
                dma((2, n_chunks)), dma((2, n_chunks)),
                dma((n_samp - 1, tiles)), dma((n_samp - 1, tiles)),
                dma((n_snp,)), dma((n_snp,)),
                dma((n_snp,)), dma((n_snp,)),
                dma((n_samp - 1,)), dma((n_samp - 1,)),
                dma((n_samp - 1,)), dma((n_samp - 1,)),
                dma((n_snp,)), dma((n_snp,)),
            ],
            compiler_params=pltpu.CompilerParams(
                collective_id=0, has_side_effects=True, vmem_limit_bytes=60 * 1024 * 1024
            ),
        )(meta, genotypes)
        snps = cols * n_snp
        return out, gram, small[0:2] * (A / snps), small[2:4, 0] / snps

    in_specs = (P("samp", "snp"), P("snp"), P("snp"), P("snp"), P("snp"), P("snp"))
    out_specs = (P("snp", None), P(), P(), P())
    return jax.shard_map(body, mesh=mesh, in_specs=in_specs, out_specs=out_specs, check_vma=False)
```

time: 221 us -> 75.4 us (0.34)
  waiting for transfers between devices: 97.7 us -> 0 us
  Pallas kernels: 0 us -> 64.2 us
  blocking collectives: 40.8 us -> 0 us
  starting transfers between devices: 32.4 us -> 0 us
  other arithmetic: 19 us -> 5.32 us
  between operations: 14.2 us -> 0.65 us
  matrix products: 12.7 us -> 0 us
    pallas_call x0 -> x1, Pallas kernels: none -> 64.2 us  [body(): pl.pallas_call(functools.partial(kernel, n_samp, n_snp, chunk), out_shape...]
    reduce_scatter x1 -> x0, waiting for transfers between devices: 62.5 us -> none  [body(): lax.psum_scatter(jnp.concatenate([tile_piece(row_start + offset * share,...]
    psum x1 -> x0, waiting for transfers between devices: 30.9 us -> none  [body(): lax.psum((gram_part, moment_part, total_part), 'snp')]
    psum x2 -> x0, blocking collectives: 30.1 us -> none  [the longest x1 18.6 us: body(): lax.psum((gram_part, moment_part, total_part), 'snp')]
    ppermute x4 -> x0, starting transfers between devices: 27.7 us -> none  [the longest x2 25.1 us: extended(): lax.ppermute(tail, axis, [(i, (i + 1) % count) for i in range(ends)])]
    dot_general x6 -> x0, matrix products: 12.7 us -> none  [the longest x4 7.27 us: tile_piece(): lax.dot_general(rows_z, cols_z, (((0,), (0,)), ((), ())), preferred_eleme...]
    all_gather x1 -> x0, blocking collectives: 10.6 us -> none  [body(): scores = lax.all_gather(part_scores, 'samp', axis=1, tiled=True)]
    reduce_sum x4 -> x0, other arithmetic: 7.41 us -> none  [the longest x1 4.52 us: body(): jnp.sum(dosage, 0)]
  transfers between devices with their start and end apart: 7 -> 0, of which waited for: 5 -> 0; matrix products, arithmetic and copies ran while one was open for 5% -> 0% of each run, Pallas kernels for 0% -> 0%
where the time goes in v1:
time: 75.4 us; the launch traced here: 74.8 us
  Pallas kernels  64.2 us (85%)
  other arithmetic  5.32 us (7%)
  local copies, waits for them, and re-layouts  4.69 us (6%)
    pallas_call x1, Pallas kernels, body(): pl.pallas_call(functools.partial(kernel, n_samp, n_snp, chunk), out_shape...  64.2 us
    unnamed x2, local copies, waits for them, and re-layouts  3.34 us
    convert_element_type x4, other arithmetic, body(): as_row = lambda x: x.astype(jnp.float32)  2.76 us

profile of v1, /device:TPU:0, one launch (start us, length us, event | category | flops | bytes accessed | tf_op | source)
XLA Modules:
  0.0 74.8 jit_solution(3803606628585574386)
XLA Ops:
  0.6 0.7 convert_element_type.12
  1.3 0.7 convert_element_type.13
  2.0 0.7 convert_element_type.14
  2.7 0.7 convert_element_type.15
  3.4 1.3 %stack.27.meta_ref = f32[8,1024]{1,0:T(8,128)} concatenate(f32[1,1024]{1,0:T(1,128)S(1)} %bitcast.5, f32[1,1024]{1,0:T(1,128)S(1)} %bitcast.6, f32[1,1024]{1,0:T(1,128)S(1)} %bitcast.7, f32[1,1024]{1,0:T(1,128)S(1)} %bitcast.8, f32[1,1024]{1,0:T(1,128)} %bitcast.9, f32[1,1024]{1,0:T(1,128)S(1)} %stack_broadcast_in_dim.3, f32[2,1024]{1,0:T(2,128)S(1)} %stack.26), dimensions={0} | concatenate | bytes 65536 | tf_op jit(solution)/shard_map/stack | solution.py:332
  4.7 64.2 %shard_map.93 = (f32[16,8192]{1,0:T(8,128)}, f32[128,128]{1,0:T(8,128)}, f32[8,128]{1,0:T(8,128)}) custom-call(f32[8,1024]{1,0:T(8,128)} %stack.27.meta_ref, s32[2048,1024]{1,0:T(8,128)} %geno_ref.1), custom_call_target="tpu_custom_call" | custom-call | tf_op jit(solution)/shard_map/pallas_call | solution.py:337
  68.9 1.2 %slice_multiply_fusion = f32[2,128]{1,0:T(2,128)} fusion(f32[8,128]{1,0:T(8,128)} %get-tuple-element.9), kind=kLoop, calls=%fused_computation.1 | loop fusion | flops 256 | bytes 2048 | tf_op jit(solution)/shard_map/mul | solution.py:381
  70.2 1.3 %multiply_reduce_fusion = f32[2]{0:T(128)} fusion(f32[8,128]{1,0:T(8,128)} %get-tuple-element.9), kind=kLoop, calls=%fused_computation | loop fusion | flops 2 | bytes 16 | tf_op jit(solution)/shard_map/div | solution.py:381
  71.5 1.9 %copy.12 = f32[16,8192]{1,0:T(8,128)} copy(f32[16,8192]{1,0:T(8,128)} %get-tuple-element.14) | data formatting | bytes 1048576
  73.4 1.5 %copy.13 = f32[128,128]{1,0:T(8,128)} copy(f32[128,128]{1,0:T(8,128)} %get-tuple-element.15) | data formatting | bytes 131072
  (2 shorter events, 0.0 us)

commit v2 on v1

--- a/solution.py
+++ b/solution.py
@@ -26,15 +26,14 @@
     n_samp, n_snp, chunk,
     meta_ref, geno_ref,
     out_ref, gram_ref, small_ref,
-    gbuf, zt, wide, labels, stat, stat_all, own, sendq, recvq,
+    gbuf, zt, wide, labels, stat, stat_all, own, sendq, recvq, fwd_out, fwd_in,
     score_parts, gs_parts, score_in, gs_in, gs_sum, score_all, gs_all, gram_rows, gram_all,
-    load_sem, stat_ss, stat_rs, lab_ss, lab_rs, halo_ss, halo_rs, tile_ss, tile_rs,
+    load_sem, stat_ss, stat_rs, lab_ss, lab_rs, halo_ss, halo_rs, tile_ss, tile_rs, fwd_ss, fwd_rs,
     a1_ss, a1_rs, a2_ss, a2_rs, b1_ss, b1_rs, b2_ss, b2_rs, c_ss, c_rs,
 ):
     rows, cols = gbuf.shape
     half = cols // 2
     share = cols // n_samp
-    tiles = recvq.shape[1]
     n_chunks = rows // chunk
     group = A // n_snp
     total = rows * n_samp
@@ -61,7 +60,17 @@
     def _(k):
         pl.semaphore_signal(barrier, inc=1, device_id={"snp": lax.rem(p + k, n_snp)}, device_id_type=pl.DeviceIdType.MESH)
 
-    pl.semaphore_wait(barrier, n_samp - 1 + n_snp - 1)
+    @pl.when(has_left)
+    def _():
+        for k in range(1, n_samp):
+            pl.semaphore_signal(barrier, inc=1, device_id={"samp": lax.rem(s + k, n_samp), "snp": left}, device_id_type=pl.DeviceIdType.MESH)
+
+    @pl.when(has_right)
+    def _():
+        for k in range(1, n_samp):
+            pl.semaphore_signal(barrier, inc=1, device_id={"samp": lax.rem(s + k, n_samp), "snp": right}, device_id_type=pl.DeviceIdType.MESH)
+
+    pl.semaphore_wait(barrier, n_samp - 1 + n_snp - 1 + (n_samp - 1) * (right - left))
 
     lab_left = remote(meta_ref.at[:, pl.ds(0, half)], labels.at[:, pl.ds(half + cols, half)], lab_ss.at[0], lab_rs.at[0], {"snp": left})
     lab_right = remote(meta_ref.at[:, pl.ds(half, half)], labels.at[:, pl.ds(0, half)], lab_ss.at[1], lab_rs.at[1], {"snp": right})
@@ -100,12 +109,12 @@
 
     @pl.when(jnp.logical_not(has_left))
     def _():
-        wide[:, 0:half] = jnp.zeros((rows, half), jnp.bfloat16)
+        wide[:, 0:share] = jnp.zeros((rows, share), jnp.bfloat16)
         labels[:, 0:half] = jnp.full((8, half), -1.0, jnp.float32)
 
     @pl.when(jnp.logical_not(has_right))
     def _():
-        wide[:, half + cols:] = jnp.zeros((rows, half), jnp.bfloat16)
+        wide[:, share + cols:] = jnp.zeros((rows, share), jnp.bfloat16)
         labels[:, half + cols:] = jnp.full((8, half), -1.0, jnp.float32)
 
     sums = stat[...]
@@ -117,11 +126,11 @@
 
     def halo_left(c):
         part = pl.ds(pl.multiple_of(c * chunk, chunk), chunk)
-        return remote(wide.at[part, pl.ds(half, half)], wide.at[part, pl.ds(half + cols, half)], halo_ss.at[0, c], halo_rs.at[0, c], {"snp": left})
+        return remote(wide.at[part, pl.ds(share, share)], wide.at[part, pl.ds(share + cols, share)], halo_ss.at[0, c], halo_rs.at[0, c], {"snp": left})
 
     def halo_right(c):
         part = pl.ds(pl.multiple_of(c * chunk, chunk), chunk)
-        return remote(wide.at[part, pl.ds(cols, half)], wide.at[part, pl.ds(0, half)], halo_ss.at[1, c], halo_rs.at[1, c], {"snp": right})
+        return remote(wide.at[part, pl.ds(cols, share)], wide.at[part, pl.ds(0, share)], halo_ss.at[1, c], halo_rs.at[1, c], {"snp": right})
 
     def halo_start(c):
         @pl.when(has_left)
@@ -139,7 +148,7 @@
             at = slice(b * 256, (b + 1) * 256)
             g = gbuf[pl.ds(start, chunk), at].astype(jnp.float32)
             z = (g - mean[:, at]) * scale[:, at]
-            wide[pl.ds(start, chunk), half + b * 256:half + (b + 1) * 256] = z.astype(jnp.bfloat16)
+            wide[pl.ds(start, chunk), share + b * 256:share + (b + 1) * 256] = z.astype(jnp.bfloat16)
             zt[at, pl.ds(start, chunk)] = z.T.astype(jnp.bfloat16)
 
         halo_start(c)
@@ -147,34 +156,65 @@
     def tile_copy(k, t):
         return remote(sendq.at[k - 1, t], recvq.at[k - 1, t], tile_ss.at[k - 1, t], tile_rs.at[k - 1, t], {"samp": lax.rem(s + k, n_samp)})
 
-    def tile_pass(inner):
-        @pl.loop(0, n_samp * tiles)
+    def column(r, u):
+        odd, high = lax.rem(r, 2), r // 2
+        second = 2 - 3 * odd + high * (2 + 3 * odd)
+        return (r if u == 0 else 1 + lax.rem(r, 3)) if u < 2 else second
+
+    def tile_pass(u, inner):
+        @pl.loop(0, n_samp)
         def _(step):
-            k = lax.rem(step // tiles + 1, n_samp)
-            t = lax.rem(step, tiles)
+            k = lax.rem(step + 1, n_samp)
             r = lax.rem(s + k, n_samp)
-            at = r * share + t * share
-            inside = jnp.logical_and(at >= half, at < half + cols)
-
-            @pl.when(inside if inner else jnp.logical_not(inside))
-            def _():
+
+            def work():
                 part = jnp.dot(
                     zt[pl.ds(pl.multiple_of(r * share, share), share), :],
-                    wide[:, pl.ds(pl.multiple_of(at, share), share)],
+                    wide[:, pl.ds(pl.multiple_of((column(r, u) + 1) * share, share), share)],
                     preferred_element_type=jnp.float32,
                 )
 
                 @pl.when(k == 0)
                 def _():
-                    own[t] = part
+                    own[u] = part
 
                 @pl.when(k > 0)
                 def _():
-                    fixed = jnp.clip(jnp.round(part * steps), -32767.0, 32767.0)
-                    sendq[k - 1, t] = fixed.astype(jnp.int32).astype(jnp.int16)
-                    tile_copy(k, t).start()
-
-    tile_pass(True)
+                    sendq[k - 1, u] = to_fixed(part)
+                    tile_copy(k, u).start()
+
+            if u < 2:
+                work()
+            else:
+                pl.when(r == 0 if inner else r > 0)(work)
+
+    def to_fixed(part):
+        return jnp.clip(jnp.round(part * steps), -32767.0, 32767.0).astype(jnp.int32).astype(jnp.int16)
+
+    def from_fixed(tile):
+        return tile.astype(jnp.int32).astype(jnp.float32)
+
+    def total_tile(u):
+        got = jnp.zeros((share, share), jnp.float32)
+        for k in range(1, n_samp):
+            tile_copy(k, u).wait()
+            got = got + from_fixed(recvq[k - 1, u])
+        return own[u] + got * (1.0 / steps)
+
+    slot = lax.rem(s, 2)
+    high = s // 2
+    step_to = high - slot * (1 - high)
+    near = {"samp": 1 + lax.rem(s, 3)}
+    far = {"samp": (2 + s) * (1 - high), "snp": jnp.clip(p + step_to, 0, n_snp - 1)}
+    far_there = jnp.logical_and(p + step_to >= 0, p + step_to < n_snp)
+    forward = (
+        remote(fwd_out.at[0], fwd_in.at[slot], fwd_ss.at[0], fwd_rs.at[slot], near),
+        remote(fwd_out.at[1], fwd_in.at[slot], fwd_ss.at[1], fwd_rs.at[slot], far),
+    )
+
+    tile_pass(1, True)
+    tile_pass(2, True)
+    tile_pass(0, True)
 
     @pl.when(has_left)
     def _():
@@ -196,8 +236,12 @@
             halo_right(c).wait_send()
             halo_left(c).wait_recv()
 
-    tile_pass(False)
-
+    tile_pass(2, False)
+
+    one_sum = total_tile(1)
+    own[1] = one_sum
+    fwd_out[0] = to_fixed(one_sum)
+    forward[0].start()
     mine = pl.multiple_of(s * share, share)
     info = meta_ref[:, pl.ds(mine, share)]
     turned = jnp.concatenate([info] + [jnp.zeros((A - 8, share), jnp.float32)], 0).T
@@ -205,29 +249,53 @@
     chi = info[4:5]
     first = (p * cols - half).astype(jnp.int32)
 
-    def add_tile(t, scores):
-        tile = own[t]
-        got = jnp.zeros((share, share), jnp.float32)
-        for k in range(1, n_samp):
-            tile_copy(k, t).wait()
-            got = got + recvq[k - 1, t].astype(jnp.int32).astype(jnp.float32)
-        corr = (tile + got * (1.0 / steps)) / total
+    def add_tile(tile, block, scores):
+        corr = tile / total
         square = corr * corr
         adjusted = square - (1.0 - square) / (total - 2)
-        at = pl.multiple_of((s + t) * share, share)
+        at = pl.multiple_of(block * share + half, share)
         lab = labels[:, pl.ds(at, share)]
         ids = (first + at + lax.broadcasted_iota(jnp.int32, (1, share), 1)).astype(jnp.float32)
         inside = (ids >= lower) & (ids <= upper) & (lab[2:3] == chrom)
         kept = jnp.where(inside, adjusted, 0.0)
         cats = lax.broadcasted_iota(jnp.int32, (A, share), 0).astype(jnp.float32)
         member = jnp.where(cats == lab[3:4], 1.0, 0.0).astype(jnp.bfloat16)
-        for _ in range(3):
+        for _ in range(2):
             piece = kept.astype(jnp.bfloat16)
             kept = kept - piece.astype(jnp.float32)
             scores = scores + lax.dot_general(member, piece, (((1,), (1,)), ((), ())), preferred_element_type=jnp.float32)
         return scores
 
-    scores = lax.fori_loop(0, tiles, add_tile, jnp.zeros((A, share), jnp.float32))
+    scores = add_tile(total_tile(0), s, jnp.zeros((A, share), jnp.float32))
+    two_sum = total_tile(2)
+    fwd_out[1] = to_fixed(two_sum)
+
+    @pl.when(far_there)
+    def _():
+        forward[1].start()
+
+    scores = add_tile(two_sum, column(s, 2), scores)
+    scores = add_tile(own[1], column(s, 1), scores)
+    forward[0].wait_send()
+
+    @pl.when(far_there)
+    def _():
+        forward[1].wait_send()
+
+    for i in range(2):
+        arrives = jnp.logical_and(jnp.logical_or(s > 0, has_left), jnp.logical_or(s < n_samp - i, has_right))
+        got = remote(fwd_out.at[i], fwd_in.at[i], fwd_ss.at[i], fwd_rs.at[i], near)
+
+        @pl.when(arrives)
+        def _():
+            got.wait_recv()
+
+        @pl.when(jnp.logical_not(arrives))
+        def _():
+            fwd_in[i] = jnp.zeros((share, share), jnp.int16)
+
+        block = 2 * ((s + 1) // 2) - 2 + i * (1 + 2 * lax.rem(s, 2))
+        scores = add_tile(from_fixed(fwd_in[i]).T * (1.0 / steps), block, scores)
 
     weights = 1.0 / jnp.sum(scores, 0, keepdims=True)
     weighted = scores * weights
@@ -325,7 +393,7 @@
         half, share = cols // 2, cols // n_samp
         chunk = 256
         n_chunks = rows // chunk
-        tiles = (cols + share) // share
+        tiles = 3
         group = A // n_snp
         as_row = lambda x: x.astype(jnp.float32)
         nothing = jnp.zeros((cols,), jnp.float32)
@@ -346,13 +414,15 @@
             scratch_shapes=[
                 pltpu.VMEM((rows, cols), jnp.int32),
                 pltpu.VMEM((cols, rows), bf16),
-                pltpu.VMEM((rows, 2 * cols), bf16),
+                pltpu.VMEM((rows, cols + 2 * share), bf16),
                 pltpu.VMEM((8, 2 * cols), f32),
                 pltpu.VMEM((2, cols), f32),
                 pltpu.VMEM((n_samp - 1, 2, cols), f32),
                 pltpu.VMEM((tiles, share, share), f32),
                 pltpu.VMEM((n_samp - 1, tiles, share, share), i16),
                 pltpu.VMEM((n_samp - 1, tiles, share, share), i16),
+                pltpu.VMEM((2, share, share), i16),
+                pltpu.VMEM((2, share, share), i16),
                 pltpu.VMEM((n_snp, group, share), f32),
                 pltpu.VMEM((n_snp, group + 8, A), f32),
                 pltpu.VMEM((n_snp, group, share), f32),
@@ -367,6 +437,7 @@
                 dma((2,)), dma((2,)),
                 dma((2, n_chunks)), dma((2, n_chunks)),
                 dma((n_samp - 1, tiles)), dma((n_samp - 1, tiles)),
+                dma((2,)), dma((2,)),
                 dma((n_snp,)), dma((n_snp,)),
                 dma((n_snp,)), dma((n_snp,)),
                 dma((n_samp - 1,)), dma((n_samp - 1,)),

time: 75.4 us -> 67.2 us (0.89)
  Pallas kernels: 64.2 us -> 56 us
    pallas_call x1, Pallas kernels: 64.2 us -> 56 us  [body(): pl.pallas_call(functools.partial(kernel, n_samp, n_snp, chunk), out_shape...]
where the time goes in v2:
time: 67.2 us; the launch traced here: 66.7 us
  Pallas kernels  56 us (83%)
  other arithmetic  5.32 us (8%)
  local copies, waits for them, and re-layouts  4.69 us (7%)
    pallas_call x1, Pallas kernels, body(): pl.pallas_call(functools.partial(kernel, n_samp, n_snp, chunk), out_shape...  56 us
    unnamed x2, local copies, waits for them, and re-layouts  3.34 us
    convert_element_type x4, other arithmetic, body(): as_row = lambda x: x.astype(jnp.float32)  2.76 us
    another operation x3, local copies, waits for them, and re-layouts, body(): jnp.stack([as_row(win_lo), as_row(win_hi), as_row(chromosome), as_row(ann...  1.35 us

profile of v2, /device:TPU:0, one launch (start us, length us, event | category | flops | bytes accessed | tf_op | source)
XLA Modules:
  0.0 66.7 jit_solution(5577961823712732190)
XLA Ops:
  0.6 0.7 %convert_element_type.12 = f32[1024]{0:T(1024)S(1)} convert(s32[1024]{0:T(1024)} %param.7) | non-fusion elementwise | flops 1024 | bytes 8192 | tf_op jit(solution)/shard_map/convert_element_type | solution.py:398
  1.3 0.7 %convert_element_type.13 = f32[1024]{0:T(1024)S(1)} convert(s32[1024]{0:T(1024)} %param.8) | non-fusion elementwise | flops 1024 | bytes 8192 | tf_op jit(solution)/shard_map/convert_element_type | solution.py:398
  2.0 0.7 %convert_element_type.14 = f32[1024]{0:T(1024)S(1)} convert(s32[1024]{0:T(1024)} %param.10) | non-fusion elementwise | flops 1024 | bytes 8192 | tf_op jit(solution)/shard_map/convert_element_type | solution.py:398
  2.7 0.7 %convert_element_type.15 = f32[1024]{0:T(1024)S(1)} convert(s32[1024]{0:T(1024)} %param.9) | non-fusion elementwise | flops 1024 | bytes 8192 | tf_op jit(solution)/shard_map/convert_element_type | solution.py:398
  3.4 1.3 %stack.27.meta_ref = f32[8,1024]{1,0:T(8,128)} concatenate(f32[1,1024]{1,0:T(1,128)S(1)} %bitcast.5, f32[1,1024]{1,0:T(1,128)S(1)} %bitcast.6, f32[1,1024]{1,0:T(1,128)S(1)} %bitcast.7, f32[1,1024]{1,0:T(1,128)S(1)} %bitcast.8, f32[1,1024]{1,0:T(1,128)} %bitcast.9, f32[1,1024]{1,0:T(1,128)S(1)} %stack_broadcast_in_dim.3, f32[2,1024]{1,0:T(2,128)S(1)} %stack.26), dimensions={0} | concatenate | bytes 65536 | tf_op jit(solution)/shard_map/stack | solution.py:400
  4.7 56.0 %shard_map.93 = (f32[16,8192]{1,0:T(8,128)}, f32[128,128]{1,0:T(8,128)}, f32[8,128]{1,0:T(8,128)}) custom-call(f32[8,1024]{1,0:T(8,128)} %stack.27.meta_ref, s32[2048,1024]{1,0:T(8,128)} %geno_ref.1), custom_call_target="tpu_custom_call" | custom-call | tf_op jit(solution)/shard_map/pallas_call | solution.py:405
  60.8 1.2 %slice_multiply_fusion = f32[2,128]{1,0:T(2,128)} fusion(f32[8,128]{1,0:T(8,128)} %get-tuple-element.9), kind=kLoop, calls=%fused_computation.1 | loop fusion | flops 256 | bytes 2048 | tf_op jit(solution)/shard_map/mul | solution.py:452
  62.0 1.3 %multiply_reduce_fusion = f32[2]{0:T(128)} fusion(f32[8,128]{1,0:T(8,128)} %get-tuple-element.9), kind=kLoop, calls=%fused_computation | loop fusion | flops 2 | bytes 16 | tf_op jit(solution)/shard_map/div | solution.py:452
  63.4 1.9 %copy.12 = f32[16,8192]{1,0:T(8,128)} copy(f32[16,8192]{1,0:T(8,128)} %get-tuple-element.14) | data formatting | bytes 1048576
  65.2 1.5 %copy.13 = f32[128,128]{1,0:T(8,128)} copy(f32[128,128]{1,0:T(8,128)} %get-tuple-element.15) | data formatting | bytes 131072
  (2 shorter events, 0.0 us)
